TPU v7x, 16 devices: a whole 2x2x2 slice. The times are simulated.
16 devices in a mesh: nodes: 16 (over z, y, x, core).
Axes of the slice: x: 2, y: 2, z: 2, core: 2. Of those that a mesh axis runs over, the one named last changes fastest.
Arguments:
- adjacency: bfloat16 [16384, 16384], P('nodes')
- features: bfloat16 [16384, 602], P('nodes')
- w_one: float32 [602, 128], replicated
- w_two: float32 [128, 41], replicated
- labels: int32 [16384], P('nodes')
- label_mask: int32 [16384], P('nodes')
Outputs:
- output 1: float32 [1], replicated
- output 2: float32 [602, 128], replicated
- output 3: float32 [128, 41], replicated
All inputs are finite; a program needn't handle non-finite values.
Results may differ from a plain program's by a relative error of at most 0.001.
Values are sent between devices in bfloat16 or wider.
A program may use at most 1 GiB of HBM per device.

v0:
```python
import functools

import jax
import jax.numpy as jnp
from jax import lax
from jax.experimental import pallas as pl
from jax.experimental.pallas import tpu as pltpu
from jax.sharding import PartitionSpec as P

MESH = pl.DeviceIdType.MESH
AXIS = 'nodes'
TREES = 4
RING = 4
STEPS = 8
COL_CONTRACT = (((1,), (1,)), ((), ()))
ROW_CONTRACT = (((0,), (0,)), ((), ()))


def tree_axis(tree, k, core, chip):
    if tree < 3:
        weight = 2 ** ((tree + k) % 3)
        return weight, lax.rem(chip // weight, 2)
    weight = (1 - core) * 2 ** k + core * 2 ** (2 - k)
    low, high = lax.rem(chip // 2 ** k, 2), lax.rem(chip // 2 ** (2 - k), 2)
    return weight, (1 - core) * low + core * high


def chip_at(tree, offset, core, chip):
    out = chip
    for k in range(3):
        weight, bit = tree_axis(tree, k, core, chip)
        out = out + lax.rem(offset // 2 ** k, 2) * weight * (1 - 2 * bit)
    return out


def early_order(place):
    pair = (place + 1) // 2
    return place + (pair * (4 - pair)) // 4 * (7 - 2 * place)


def unit_at(tree, offset, core, chip):
    return (chip_at(tree, offset, core, chip) * 2 + core) * TREES + tree


def neighbour(tree, k, core, chip):
    weight, bit = tree_axis(tree, k, core, chip)
    return (chip + weight * (1 - 2 * bit)) * 2 + core


def remote(src, dst, send_sem, recv_sem, device):
    return pltpu.make_async_remote_copy(src_ref=src, dst_ref=dst, send_sem=send_sem, recv_sem=recv_sem, device_id=(device,), device_id_type=MESH)


def place():
    me = lax.axis_index(AXIS)
    core, chip = lax.rem(me, 2), me // 2
    return me, core, chip, chip * 2 + 1 - core


def gather_send(buf, sems, tree, offset, k, unit, rows=slice(None)):
    send, recv, hand = sems
    me, core, chip, partner = place()
    ref = buf.at[unit, rows]
    remote(ref, ref, send, recv.at[offset + 2 ** k - 1, tree], neighbour(tree, k, core, chip)).start()


def gather_hand(buf, sems, slot, unit):
    send, recv, hand = sems
    me, core, chip, partner = place()
    remote(buf.at[unit], buf.at[unit], send, hand.at[slot], partner).start()


def gather_start(buf, sems, links):
    me = lax.axis_index(AXIS)
    for k in range(links):
        for t in range(TREES):
            gather_send(buf, sems, t, 0, k, me * TREES + t)
        if k == 0:
            for t in range(TREES):
                gather_hand(buf, sems, 0, me * TREES + t)


def gather_arrive(buf, sems, s, links, trees=range(TREES), slot=None, cut=None):
    send, recv, hand = sems
    me, core, chip, partner = place()
    units = {t: unit_at(t, s, core, chip) for t in trees}
    for t, u in units.items():
        remote(buf.at[u], buf.at[u], send, recv.at[s - 1, t], partner).wait_recv()
        split = cut is not None and t == TREES - 1

        @pl.when(s == 1)
        def _():
            gather_send(buf, sems, t, s, 1, u)

        @pl.when((s > 1) & (s < (3 if split else 4)))
        def _():
            gather_send(buf, sems, t, s, 2, u)
        if split:
            @pl.when(s == 3)
            def _():
                gather_send(buf, sems, t, s, 2, u, slice(0, cut))

            @pl.when(s == 5)
            def _():
                gather_send(buf, sems, t, s, 1, u, slice(cut, None))
        gather_hand(buf, sems, s if slot is None else slot, u)

    @pl.when(s == 1)
    def _():
        if links < 3:
            for t in range(TREES):
                gather_send(buf, sems, t, 0, 2, me * TREES + t)
        for t, u in units.items():
            gather_send(buf, sems, t, s, 2, u)


def gather_take(buf, sems, slot, count=TREES):
    send, recv, hand = sems
    me, core, chip, partner = place()
    units = buf.at[pl.ds(0, count)]
    remote(units, units, send, hand.at[slot], partner).wait_recv()


def gather_drain(buf, sems):
    send, recv, hand = sems
    me, core, chip, partner = place()
    sent = buf.at[pl.ds(0, TREES * (STEPS - 1 + STEPS))]
    remote(sent, sent, send, hand.at[0], partner).wait_send()


def gather_sems():
    dma = pltpu.SemaphoreType.DMA
    return [dma, dma((STEPS - 1, TREES)), dma((STEPS + 1,))]


def barrier_near():
    me, core, chip, partner = place()
    sem = pltpu.get_barrier_semaphore()
    pl.semaphore_signal(sem, inc=1, device_id=(partner,), device_id_type=MESH)
    for k in range(3):
        pl.semaphore_signal(sem, inc=1, device_id=(neighbour(0, k, core, chip),), device_id_type=MESH)
    pl.semaphore_wait(sem, 4)


def send_all(n, src, dst, send_sem, recv_sem):
    me = lax.axis_index(AXIS)
    for i in range(1, n):
        to = lax.rem(me + i, n)
        remote(src(to), dst, send_sem, recv_sem, to).start()


def wait_all(ref, send_sem, recv_sem):
    me, core, chip, partner = place()
    copy = remote(ref, ref, send_sem, recv_sem, partner)
    copy.wait_send()
    copy.wait_recv()


def step_kernel(n, x_ref, w_hbm, w2t_ref, y_ref, m_ref, adj, loss_ref, dw_ref, dw2_ref,
                ring, buf, acc, h_buf, s_one, z_one, u_two, w_v, small, count, stage, mine, total, child, part, parts, whole,
                small_parts, small_whole, pair, g_two, g_one, picked,
                ring_sem, x_sem, w_sem, count_send, count_recv, dsend, drecv, csend, crecv, fsend, frecv, gsend, grecv,
                ssend, srecv, bsend, brecv, psend, precv, qsend, qrecv, *sems):
    me, core, chip, partner = place()
    sems_x, sems_h = sems[:3], sems[3:]
    width = buf.shape[2]
    feats, rows = acc.shape
    hidden = h_buf.shape[1]
    chunks = [slice(t * width, (t + 1) * width) for t in range(TREES)]

    def slab(s, slot, j):
        u = unit_at(j % TREES, s, core if j < TREES else 1 - core, chip)
        return pltpu.make_async_copy(adj.at[:, pl.ds(pl.multiple_of(u * width, width), width)], ring.at[slot * 8 + j], ring_sem.at[slot, j // TREES])

    def load(s, slot, half):
        for t in range(TREES):
            slab(s, slot, half * TREES + t).start()

    def loaded(slot, half):
        four = ring.at[pl.ds(0, TREES)]
        pltpu.make_async_copy(four, four, ring_sem.at[slot, half]).wait()

    with jax.named_scope('start'):
        fetch = [pltpu.make_async_copy(x_ref.at[:, pl.ds(t * width, width)], buf.at[me * TREES + t], x_sem) for t in range(TREES)]
        for copy in fetch:
            copy.start()
        weight = m_ref[...].astype(jnp.float32)
        count[me] = jnp.broadcast_to(jnp.sum(weight, axis=1, keepdims=True), count.shape[1:])
        barrier_near()
        four = buf.at[pl.ds(0, TREES)]
        pltpu.make_async_copy(four, four, x_sem).wait()
    gather_start(buf, sems_x, 2)
    weights = pltpu.make_async_copy(w_hbm, w_v, w_sem)
    weights.start()
    for s in range(RING):
        for half in range(2):
            load(s, s, half)
    acc[...] = jnp.zeros_like(acc)

    def terms(units_ref, s, slot, half, trees=range(TREES)):
        which = core if half == 0 else 1 - core
        return [(units_ref, unit_at(t, s, which, chip), slot * 8 + half * TREES + t) for t in trees]

    def aggregate(out, pairs):
        for cols in chunks:
            out[:, cols] += sum(lax.dot_general(ref[u], ring[j, cols], COL_CONTRACT, preferred_element_type=jnp.float32) for ref, u, j in pairs)

    def step_one(s, carry):
        with jax.named_scope('arrive'):
            @pl.when(s > 0)
            def _():
                gather_arrive(buf, sems_x, s, 2, cut=cut)
        for half in range(2):
            with jax.named_scope('consume'):
                if half == 1:
                    gather_take(buf, sems_x, s)
                slot = lax.rem(s, RING)
                loaded(slot, half)
                aggregate(acc, terms(buf, s, slot, half))
                late = s // RING
                load((1 - late) * (s + RING) + late * early_order(s - late * RING), slot, half)
        return carry

    cut = feats * 2 // 3 // 16 * 16
    final, slot = STEPS - 1, (STEPS - 1) % RING
    lax.fori_loop(0, final, step_one, 0)
    early, late = (range(TREES - 1), final), (range(TREES - 1, TREES), STEPS)
    for half in range(2):
        for trees, hand in (early, late):
            with jax.named_scope('consume'):
                if half == 0:
                    gather_arrive(buf, sems_x, final, 2, trees, hand, cut)
                else:
                    gather_take(buf, sems_x, hand, len(trees))
                if hand == final:
                    loaded(slot, half)
                aggregate(acc, terms(buf, final, slot, half, trees))
    for half in range(2):
        load(early_order(final - RING), slot, half)
    with jax.named_scope('mid'):
        weights.wait()
        s_one[0:feats] = acc[...].astype(jnp.bfloat16)
        s_one[feats:] = jnp.zeros_like(s_one[feats:])
        w_rows = w_v[...].astype(jnp.bfloat16)
        for t, cols in enumerate(chunks):
            z = lax.dot_general(w_rows, s_one[0:feats, cols], ROW_CONTRACT, preferred_element_type=jnp.float32)
            z_one[:, cols] = z
            h_buf[me * TREES + t] = jnp.maximum(z, 0.0).astype(jnp.bfloat16)
    gather_start(h_buf, sems_h, 3)
    send_all(n, lambda to: count.at[me], count.at[me], count_send, count_recv)
    two = acc.at[0:hidden]

    def take_two(p, half):
        loaded(lax.rem(p, RING), half)
        return terms(h_buf, early_order(p), lax.rem(p, RING), half)

    def back_order(i):
        return early_order(STEPS - 1 - i)

    def load_two(p, half):
        late = p // RING
        load((1 - late) * early_order(p + RING - late * RING) + late * back_order(p - late * RING), lax.rem(p, RING), half)

    two[...] = jnp.zeros_like(two)
    with jax.named_scope('consume'):
        aggregate(two, take_two(0, 0))
        load_two(0, 0)
        gather_take(h_buf, sems_h, 0)
        aggregate(two, take_two(0, 1))
        load_two(0, 1)
    with jax.named_scope('arrive'):
        gather_arrive(h_buf, sems_h, 1, 3)
    with jax.named_scope('consume'):
        aggregate(two, take_two(1, 0))
        load_two(1, 0)

    for p in range(2, STEPS):
        with jax.named_scope('arrive'):
            gather_arrive(h_buf, sems_h, early_order(p), 3)
            gather_take(h_buf, sems_h, early_order(p - 1))
        with jax.named_scope('consume'):
            aggregate(two, take_two(p - 1, 1) + take_two(p, 0))
            load_two(p - 1, 1)
            load_two(p, 0)
    with jax.named_scope('last'):
        gather_take(h_buf, sems_h, STEPS - 1)
        aggregate(two, take_two(STEPS - 1, 1))
        load_two(STEPS - 1, 1)
    with jax.named_scope('soft'):
        wait_all(count.at[pl.ds(0, n - 1)], count_send, count_recv)
        labelled = jnp.sum(count[...], axis=0)[0:1, 0:1]
        s_two = two[...].astype(jnp.bfloat16)
        w_two = w2t_ref[...].astype(jnp.bfloat16)
        logits = jnp.dot(w_two, s_two, preferred_element_type=jnp.float32)
        shifted = logits - jnp.max(logits, axis=0, keepdims=True)
        log_prob = shifted - jnp.log(jnp.sum(jnp.exp(shifted), axis=0, keepdims=True))
        hot = lax.broadcasted_iota(jnp.int32, logits.shape, 0) == y_ref[...]
        grad = (weight * (jnp.exp(log_prob) - hot.astype(jnp.float32)) / labelled).astype(jnp.bfloat16)
        u_two[...] = lax.dot_general(w_two, grad, ROW_CONTRACT, preferred_element_type=jnp.float32).astype(jnp.bfloat16)
        g_two[...] = grad
        picked[...] = -weight * jnp.sum(jnp.where(hot, log_prob, 0.0), axis=0, keepdims=True)
    classes = g_two.shape[0]
    edge = small.shape[0] - 8
    owners = small.shape[0] // 8
    tile = pl.ds(pl.multiple_of(me * 8, 8), 8)

    def send_small():
        loss = jnp.sum(picked[...], axis=1, keepdims=True)
        labelled = jnp.sum(count[...], axis=0)[0:1, 0:1]
        small[0:classes] = lax.dot_general(g_two[...], two[...].astype(jnp.bfloat16), COL_CONTRACT, preferred_element_type=jnp.float32)
        small[classes:edge] = jnp.zeros((edge - classes, hidden), jnp.float32)
        small[edge:] = jnp.broadcast_to(loss / labelled, (8, hidden))
        for o in range(owners):
            @pl.when(me != o)
            def _():
                remote(small.at[pl.ds(o * 8, 8)], small_parts.at[me], ssend, srecv, o).start()

    def to_partner(s, t):
        return remote(stage.at[s, t], total.at[s, t], dsend, drecv.at[s], partner)

    def to_parent(s, t, k):
        return remote(total.at[s, t], child.at[s - 1, t], csend, crecv.at[s - 1, t], neighbour(t, k, core, chip))

    def reduce_small():
        @pl.when(me < owners)
        def _():
            small_parts[me] = small[tile]
            got = small_parts.at[pl.ds(0, n - 1)]
            remote(got, got, ssend, srecv, partner).wait_recv()
            small_whole[tile] = jnp.sum(small_parts[...], axis=0)
            for i in range(1, n):
                remote(small_whole.at[tile], small_whole.at[tile], bsend, brecv, lax.rem(me + i, n)).start()

    def finish_small():
        sent = small_parts.at[pl.ds(0, n - 1)]
        fewer, every = small_whole.at[pl.ds(0, owners * 8 - 8)], small_whole.at[pl.ds(0, owners * 8)]

        @pl.when(me < owners)
        def _():
            remote(sent, sent, bsend, brecv, partner).wait_send()
            remote(fewer, fewer, ssend, brecv, partner).wait_send()
            remote(fewer, fewer, ssend, brecv, partner).wait_recv()

        @pl.when(me >= owners)
        def _():
            remote(every, every, ssend, brecv, partner).wait_send()
            remote(every, every, ssend, brecv, partner).wait_recv()

    def give(s, slot):
        loaded(slot, 1)
        for t in range(TREES):
            stage[s, t] = jnp.dot(u_two[...], ring[slot * 8 + TREES + t], preferred_element_type=jnp.float32)
        for t in range(TREES):
            to_partner(s, t).start()
        loaded(slot, 0)
        for t in range(TREES):
            mine[t] = jnp.dot(u_two[...], ring[slot * 8 + t], preferred_element_type=jnp.float32)

    def join(s):
        remote(total.at[s], total.at[s], dsend, drecv.at[s], partner).wait_recv()

    def gather_children(s, t):
        total[s, t] = total[s, t] + mine[t]
        for k in range(3):
            @pl.when(s < 2 ** k)
            def _():
                to_parent(s + 2 ** k, t, k).wait_recv()
                total[s, t] = total[s, t] + child[s + 2 ** k - 1, t]

    def step_back(i, carry):
        s = back_order(i)
        slot = lax.rem(i, RING)
        with jax.named_scope('give'):
            give(s, slot)

            @pl.when(i + RING < STEPS)
            def _():
                load(back_order(i + RING), slot, 1)
                load(back_order(i + RING), slot, 0)

            @pl.when(i == 0)
            def _():
                send_small()
        with jax.named_scope('take'):
            join(s)
            for t in range(TREES):
                gather_children(s, t)
                for k in range(3):
                    @pl.when((s >= 2 ** k) & (s < 2 ** (k + 1)))
                    def _():
                        to_parent(s, t, k).start()
        return carry

    lax.fori_loop(0, STEPS - 1, step_back, 0)
    chips = n // 2
    half, share = part.shape[0] // 2, part.shape[0] // n
    mine_rows = pl.ds(pl.multiple_of(core * half, 8), half)
    their_rows = pl.ds(pl.multiple_of((1 - core) * half, 8), half)
    most = slice(0, (TREES - 1) * width)
    with jax.named_scope('give'):
        give(0, (STEPS - 1) % RING)
        join(0)

    def hidden_grad(t):
        gather_children(0, t)
        g_one[:, chunks[t]] = jnp.where(z_one[:, chunks[t]] > 0.0, total[0, t], 0.0).astype(jnp.bfloat16)

    def weight_grad(out_rows, cols):
        return lax.dot_general(s_one[out_rows, cols], g_one[:, cols], COL_CONTRACT, preferred_element_type=jnp.float32)

    with jax.named_scope('take'):
        for t in range(TREES - 1):
            hidden_grad(t)
        part[...] = weight_grad(slice(None), most)
        hidden_grad(TREES - 1)
    with jax.named_scope('dw'):
        part[their_rows] = part[their_rows] + weight_grad(their_rows, chunks[-1])
        over = remote(part.at[their_rows], pair, psend, precv, partner)
        over.start()
        part[mine_rows] = part[mine_rows] + weight_grad(mine_rows, chunks[-1])
    reduce_small()
    with jax.named_scope('drain'):
        gather_drain(buf, sems_x)
        gather_drain(h_buf, sems_h)
        remote(stage, stage, dsend, drecv.at[0], partner).wait_send()
        remote(child, child, csend, crecv.at[0, 0], partner).wait_send()
    with jax.named_scope('pair'):
        over.wait()
        pair[...] = pair[...] + part[mine_rows]

    def share_of(q):
        return pl.ds(pl.multiple_of(q * share, 8), share)

    for i in range(1, chips):
        to = lax.rem(chip + i, chips)
        remote(pair.at[share_of(to)], parts.at[chip], fsend, frecv, to * 2 + core).start()
    parts[chip] = pair[share_of(chip)]
    with jax.named_scope('red'):
        wait_all(parts.at[pl.ds(0, chips - 1)], fsend, frecv)
    own = whole.at[pl.ds(pl.multiple_of(core * half + chip * share, 8), share)]
    own[...] = jnp.sum(parts[...], axis=0)
    for i in range(1, chips):
        remote(own, own, gsend, grecv, lax.rem(chip + i, chips) * 2 + core).start()
    with jax.named_scope('spread'):
        wait_all(whole.at[pl.ds(0, (chips - 1) * share)], gsend, grecv)
    swap = remote(whole.at[mine_rows], whole.at[mine_rows], qsend, qrecv, partner)
    swap.start()
    finish_small()
    dw2_ref[...] = small_whole[0:dw2_ref.shape[0]]
    loss_ref[...] = small_whole[edge:edge + 8]
    with jax.named_scope('swap'):
        swap.wait()
    dw_ref[...] = whole[0:feats]


def finish_kernel(loss_in, dw_in, dw2_in, loss_ref, dw_ref, dw2_ref):
    loss_ref[...] = loss_in[0:1, 0:1]
    dw_ref[...] = dw_in[...]
    dw2_ref[...] = dw2_in[...]


def train_step(x_rows, w_one, w2t, labels, mask, adj):
    rows, nodes = adj.shape
    n = nodes // rows
    feats, width = x_rows.shape[0], rows // TREES
    classes, hidden = w2t.shape
    units = n * TREES
    small = -(-classes // 8) * 8 + 8
    share = -(-feats // (8 * n)) * 8
    vmem, hbm = pl.BlockSpec(memory_space=pltpu.VMEM), pl.BlockSpec(memory_space=pl.ANY)
    dma, f32, bf16 = pltpu.SemaphoreType.DMA, jnp.float32, jnp.bfloat16
    block = (TREES, hidden, width)
    loss, dw_one, dw_two = pl.pallas_call(
        functools.partial(step_kernel, n),
        name='step',
        out_shape=(pltpu.VMEM((8, hidden), f32), pltpu.VMEM((feats, hidden), f32), pltpu.VMEM((classes, hidden), f32)),
        in_specs=[hbm, hbm, vmem, vmem, vmem, hbm],
        out_specs=(vmem,) * 3,
        scratch_shapes=[
            pltpu.VMEM((RING * 8, rows, width), bf16), pltpu.VMEM((units, feats, width), bf16), pltpu.VMEM((feats, rows), f32),
            pltpu.VMEM((units, hidden, width), bf16), pltpu.VMEM((n * share, rows), bf16), pltpu.VMEM((hidden, rows), f32),
            pltpu.VMEM((hidden, rows), bf16), pltpu.VMEM((feats, hidden), f32), pltpu.VMEM((small, hidden), f32), pltpu.VMEM((n, 8, 128), f32),
            pltpu.VMEM((STEPS, *block), f32), pltpu.VMEM(block, f32), pltpu.VMEM((STEPS, *block), f32), pltpu.VMEM((STEPS - 1, *block), f32),
            pltpu.VMEM((n * share, hidden), f32), pltpu.VMEM((n // 2, share, hidden), f32), pltpu.VMEM((n * share, hidden), f32),
            pltpu.VMEM((n, 8, hidden), f32), pltpu.VMEM((small, hidden), f32), pltpu.VMEM((n // 2 * share, hidden), f32),
            pltpu.VMEM((classes, rows), bf16), pltpu.VMEM((hidden, rows), bf16), pltpu.VMEM((1, rows), f32),
            dma((RING, 2)), dma, dma, dma, dma, dma, dma((STEPS,)), dma, dma((STEPS - 1, TREES)), *[dma] * 12, *gather_sems(), *gather_sems()],
        compiler_params=pltpu.CompilerParams(collective_id=0, has_side_effects=True, vmem_limit_bytes=62000000),
        cost_estimate=pl.CostEstimate(flops=2 * rows * nodes * (feats + 2 * hidden), bytes_accessed=6 * rows * nodes, transcendentals=0),
    )(x_rows, w_one, w2t, labels, mask, adj)
    return pl.pallas_call(
        finish_kernel,
        name='finish',
        out_shape=(jax.ShapeDtypeStruct((1, 1), f32), jax.ShapeDtypeStruct((feats, hidden), f32), jax.ShapeDtypeStruct((classes, hidden), f32)),
        in_specs=[vmem] * 3,
        out_specs=(vmem,) * 3,
    )(*[pltpu.with_memory_space_constraint(x, pltpu.VMEM) for x in (loss, dw_one, dw_two)])


def solution(mesh):
    axis_name = AXIS

    def local_step(adj_rows, feat_rows, w_one, w_two, label_rows, mask_rows):
        rows = adj_rows.shape[0]
        loss, dw_one, dw_two = train_step(feat_rows.T, w_one, w_two.T, label_rows.reshape(1, rows), mask_rows.reshape(1, rows), adj_rows)
        return loss.reshape(1), dw_one, dw_two.T

    return jax.shard_map(local_step, mesh=mesh, in_specs=(P(axis_name, None), P(axis_name, None), P(None, None), P(None, None), P(axis_name), P(axis_name)), out_specs=(P(None), P(None, None), P(None, None)), check_vma=False)
```

profile of v0, /device:TPU:0, one launch (start us, length us, event | category | flops | bytes accessed | tf_op | source)
XLA Modules:
  0.0 135.5 jit_solution(14265700566754622976)
XLA Ops:
  0.6 134.1 %step.1 = (f32[8,128]{1,0:T(8,128)S(1)}, f32[602,128]{1,0:T(8,128)S(1)}, f32[41,128]{1,0:T(8,128)S(1)}) custom-call(bf16[602,1024]{1,0:T(8,128)(2,1)} %bitcast.6, f32[602,128]{1,0:T(8,128)} %w_hbm.1, f32[41,128]{1,0:T(8,128)} %bitcast.7, s32[1,1024]{1,0:T(1,128)} %bitcast.9, s32[1,1024]{1,0:T(1,128)} %bitcast.10, bf16[1024,16384]{1,0:T(8,128)(2,1)} %adj.1), custom_call_target="tpu_custom_call" | custom-call | flops 28789702656 | bytes 100663296 | tf_op jit(solution)/shard_map/step/pallas_call | solution.py:473
  134.7 0.7 finish.1
where the time goes:
time: 136 us; the launch traced here: 135 us
  Pallas kernels  135 us (99%)
    pallas_call x1, Pallas kernels, train_step(): pl.pallas_call(functools.partial(step_kernel, n), name='step', out_shape=...  134 us

commit v1 on v0

--- a/solution.py
+++ b/solution.py
@@ -160,7 +160,7 @@
                 ring, buf, acc, h_buf, s_one, z_one, u_two, w_v, small, count, stage, mine, total, child, part, parts, whole,
                 small_parts, small_whole, pair, g_two, g_one, picked,
                 ring_sem, x_sem, w_sem, count_send, count_recv, dsend, drecv, csend, crecv, fsend, frecv, gsend, grecv,
-                ssend, srecv, bsend, brecv, psend, precv, qsend, qrecv, *sems):
+                ssend, srecv, bsend, brecv, psend, precv, qsend, qrecv, cut_sem, *sems):
     me, core, chip, partner = place()
     sems_x, sems_h = sems[:3], sems[3:]
     width = buf.shape[2]
@@ -346,6 +346,18 @@
             remote(every, every, ssend, brecv, partner).wait_send()
             remote(every, every, ssend, brecv, partner).wait_recv()
 
+    far, edge_row = STEPS - 2, hidden * 2 // 3 // 8 * 8 + 8
+
+    def from_far_to(which):
+        rows, k = ((slice(0, edge_row), 2), (slice(edge_row, hidden), 1))[which]
+        sem = cut_sem if which else crecv.at[far - 1, TREES - 1]
+        return remote(total.at[far, TREES - 1, rows], child.at[far - 1, TREES - 1, rows], csend, sem, neighbour(TREES - 1, k, core, chip))
+
+    def add_far(s, which):
+        from_far_to(which).wait_recv()
+        rows = (slice(0, edge_row), slice(edge_row, hidden))[which]
+        total[s, TREES - 1, rows] = total[s, TREES - 1, rows] + child[far - 1, TREES - 1, rows]
+
     def give(s, slot):
         loaded(slot, 1)
         for t in range(TREES):
@@ -362,10 +374,17 @@
     def gather_children(s, t):
         total[s, t] = total[s, t] + mine[t]
         for k in range(3):
-            @pl.when(s < 2 ** k)
+            skip = far - 4 if k == 2 and t == TREES - 1 else STEPS
+
+            @pl.when((s < 2 ** k) & (s != skip))
             def _():
                 to_parent(s + 2 ** k, t, k).wait_recv()
                 total[s, t] = total[s, t] + child[s + 2 ** k - 1, t]
+        if t == TREES - 1:
+            for which, parent in ((0, far - 4), (1, far - 2)):
+                @pl.when(s == parent)
+                def _():
+                    add_far(s, which)
 
     def step_back(i, carry):
         s = back_order(i)
@@ -386,9 +405,16 @@
             for t in range(TREES):
                 gather_children(s, t)
                 for k in range(3):
-                    @pl.when((s >= 2 ** k) & (s < 2 ** (k + 1)))
+                    skip = far if k == 2 and t == TREES - 1 else STEPS
+
+                    @pl.when((s >= 2 ** k) & (s < 2 ** (k + 1)) & (s != skip))
                     def _():
                         to_parent(s, t, k).start()
+                if t == TREES - 1:
+                    @pl.when(s == far)
+                    def _():
+                        from_far_to(0).start()
+                        from_far_to(1).start()
         return carry
 
     lax.fori_loop(0, STEPS - 1, step_back, 0)
@@ -484,7 +510,7 @@
             pltpu.VMEM((n * share, hidden), f32), pltpu.VMEM((n // 2, share, hidden), f32), pltpu.VMEM((n * share, hidden), f32),
             pltpu.VMEM((n, 8, hidden), f32), pltpu.VMEM((small, hidden), f32), pltpu.VMEM((n // 2 * share, hidden), f32),
             pltpu.VMEM((classes, rows), bf16), pltpu.VMEM((hidden, rows), bf16), pltpu.VMEM((1, rows), f32),
-            dma((RING, 2)), dma, dma, dma, dma, dma, dma((STEPS,)), dma, dma((STEPS - 1, TREES)), *[dma] * 12, *gather_sems(), *gather_sems()],
+            dma((RING, 2)), dma, dma, dma, dma, dma, dma((STEPS,)), dma, dma((STEPS - 1, TREES)), *[dma] * 13, *gather_sems(), *gather_sems()],
         compiler_params=pltpu.CompilerParams(collective_id=0, has_side_effects=True, vmem_limit_bytes=62000000),
         cost_estimate=pl.CostEstimate(flops=2 * rows * nodes * (feats + 2 * hidden), bytes_accessed=6 * rows * nodes, transcendentals=0),
     )(x_rows, w_one, w2t, labels, mask, adj)

time: 136 us -> 135 us (level)
  no operation moved by 1% of the time
where the time goes in v1:
time: 135 us
  Pallas kernels  134 us (99%)
    pallas_call x1, Pallas kernels, train_step(): pl.pallas_call(functools.partial(step_kernel, n), name='step', out_shape=...  134 us

profile of v1, /device:TPU:0, one launch (start us, length us, event | category | flops | bytes accessed | tf_op | source)
XLA Modules:
  0.0 134.9 jit_solution(11462018188467467968)
XLA Ops:
  0.6 133.5 %step.1 = (f32[8,128]{1,0:T(8,128)S(1)}, f32[602,128]{1,0:T(8,128)S(1)}, f32[41,128]{1,0:T(8,128)S(1)}) custom-call(bf16[602,1024]{1,0:T(8,128)(2,1)} %bitcast.6, f32[602,128]{1,0:T(8,128)} %w_hbm.1, f32[41,128]{1,0:T(8,128)} %bitcast.7, s32[1,1024]{1,0:T(1,128)} %bitcast.9, s32[1,1024]{1,0:T(1,128)} %bitcast.10, bf16[1024,16384]{1,0:T(8,128)(2,1)} %adj.1), custom_call_target="tpu_custom_call" | custom-call | flops 28789702656 | bytes 100663296 | tf_op jit(solution)/shard_map/step/pallas_call | solution.py:499
  134.2 0.7 finish.1

commit v2 on v1

--- a/solution.py
+++ b/solution.py
@@ -57,72 +57,84 @@
     return me, core, chip, chip * 2 + 1 - core
 
 
-def gather_send(buf, sems, tree, offset, k, unit, rows=slice(None)):
-    send, recv, hand = sems
+def gather_send(buf, sems, tree, offset, k, unit, rows=slice(None), last=False):
+    send, recv, late, hand = sems
     me, core, chip, partner = place()
     ref = buf.at[unit, rows]
-    remote(ref, ref, send, recv.at[offset + 2 ** k - 1, tree], neighbour(tree, k, core, chip)).start()
+    got = late.at[4] if last else late.at[offset] if k == 2 else recv.at[offset + 2 ** k - 1, tree]
+    remote(ref, ref, send, got, neighbour(tree, k, core, chip)).start()
 
 
 def gather_hand(buf, sems, slot, unit):
-    send, recv, hand = sems
+    send, recv, late, hand = sems
     me, core, chip, partner = place()
     remote(buf.at[unit], buf.at[unit], send, hand.at[slot], partner).start()
 
 
-def gather_start(buf, sems, links):
+def gather_start(buf, sems, early):
     me = lax.axis_index(AXIS)
-    for k in range(links):
-        for t in range(TREES):
+    for k in range(3):
+        for t in range(TREES if k < 2 else early):
             gather_send(buf, sems, t, 0, k, me * TREES + t)
         if k == 0:
             for t in range(TREES):
                 gather_hand(buf, sems, 0, me * TREES + t)
 
 
-def gather_arrive(buf, sems, s, links, trees=range(TREES), slot=None, cut=None):
-    send, recv, hand = sems
+def gather_arrive(buf, sems, s, early, trees=range(TREES), slot=None, cut=None):
+    send, recv, late, hand = sems
     me, core, chip, partner = place()
     units = {t: unit_at(t, s, core, chip) for t in trees}
-    for t, u in units.items():
-        remote(buf.at[u], buf.at[u], send, recv.at[s - 1, t], partner).wait_recv()
-        split = cut is not None and t == TREES - 1
-
-        @pl.when(s == 1)
-        def _():
-            gather_send(buf, sems, t, s, 1, u)
-
-        @pl.when((s > 1) & (s < (3 if split else 4)))
-        def _():
-            gather_send(buf, sems, t, s, 2, u)
-        if split:
-            @pl.when(s == 3)
-            def _():
-                gather_send(buf, sems, t, s, 2, u, slice(0, cut))
-
+    slot = s if slot is None else slot
+
+    @pl.when(s < 4)
+    def _():
+        for t, u in units.items():
+            remote(buf.at[u], buf.at[u], send, recv.at[s - 1, t], partner).wait_recv()
+            split = cut is not None and t == TREES - 1
+
+            @pl.when(s == 1)
+            def _():
+                gather_send(buf, sems, t, s, 1, u)
+
+            @pl.when((s > 1) & (s < (3 if split else 4)))
+            def _():
+                gather_send(buf, sems, t, s, 2, u)
+            if split:
+                @pl.when(s == 3)
+                def _():
+                    gather_send(buf, sems, t, s, 2, u, slice(0, cut), True)
+            gather_hand(buf, sems, slot, u)
+
+    @pl.when(s >= 4)
+    def _():
+        some = buf.at[pl.ds(0, len(units))]
+        which = late.at[s - 4] if len(units) > 1 else late.at[4]
+        remote(some, some, send, which, partner).wait_recv()
+        if cut is not None and TREES - 1 in units:
             @pl.when(s == 5)
             def _():
-                gather_send(buf, sems, t, s, 1, u, slice(cut, None))
-        gather_hand(buf, sems, s if slot is None else slot, u)
+                gather_send(buf, sems, TREES - 1, s, 1, units[TREES - 1], slice(cut, None), True)
+        for u in units.values():
+            gather_hand(buf, sems, slot, u)
 
     @pl.when(s == 1)
     def _():
-        if links < 3:
-            for t in range(TREES):
-                gather_send(buf, sems, t, 0, 2, me * TREES + t)
+        for t in range(early, TREES):
+            gather_send(buf, sems, t, 0, 2, me * TREES + t)
         for t, u in units.items():
             gather_send(buf, sems, t, s, 2, u)
 
 
 def gather_take(buf, sems, slot, count=TREES):
-    send, recv, hand = sems
+    send, recv, late, hand = sems
     me, core, chip, partner = place()
     units = buf.at[pl.ds(0, count)]
     remote(units, units, send, hand.at[slot], partner).wait_recv()
 
 
 def gather_drain(buf, sems):
-    send, recv, hand = sems
+    send, recv, late, hand = sems
     me, core, chip, partner = place()
     sent = buf.at[pl.ds(0, TREES * (STEPS - 1 + STEPS))]
     remote(sent, sent, send, hand.at[0], partner).wait_send()
@@ -130,7 +142,7 @@
 
 def gather_sems():
     dma = pltpu.SemaphoreType.DMA
-    return [dma, dma((STEPS - 1, TREES)), dma((STEPS + 1,))]
+    return [dma, dma((3, TREES)), dma((5,)), dma((STEPS + 1,))]
 
 
 def barrier_near():
@@ -162,7 +174,7 @@
                 ring_sem, x_sem, w_sem, count_send, count_recv, dsend, drecv, csend, crecv, fsend, frecv, gsend, grecv,
                 ssend, srecv, bsend, brecv, psend, precv, qsend, qrecv, cut_sem, *sems):
     me, core, chip, partner = place()
-    sems_x, sems_h = sems[:3], sems[3:]
+    sems_x, sems_h = sems[:4], sems[4:]
     width = buf.shape[2]
     feats, rows = acc.shape
     hidden = h_buf.shape[1]
@@ -189,7 +201,7 @@
         barrier_near()
         four = buf.at[pl.ds(0, TREES)]
         pltpu.make_async_copy(four, four, x_sem).wait()
-    gather_start(buf, sems_x, 2)
+    gather_start(buf, sems_x, 0)
     weights = pltpu.make_async_copy(w_hbm, w_v, w_sem)
     weights.start()
     for s in range(RING):
@@ -209,7 +221,7 @@
         with jax.named_scope('arrive'):
             @pl.when(s > 0)
             def _():
-                gather_arrive(buf, sems_x, s, 2, cut=cut)
+                gather_arrive(buf, sems_x, s, 0, cut=cut)
         for half in range(2):
             with jax.named_scope('consume'):
                 if half == 1:
@@ -229,7 +241,7 @@
         for trees, hand in (early, late):
             with jax.named_scope('consume'):
                 if half == 0:
-                    gather_arrive(buf, sems_x, final, 2, trees, hand, cut)
+                    gather_arrive(buf, sems_x, final, 0, trees, hand, cut)
                 else:
                     gather_take(buf, sems_x, hand, len(trees))
                 if hand == final:
@@ -246,7 +258,7 @@
             z = lax.dot_general(w_rows, s_one[0:feats, cols], ROW_CONTRACT, preferred_element_type=jnp.float32)
             z_one[:, cols] = z
             h_buf[me * TREES + t] = jnp.maximum(z, 0.0).astype(jnp.bfloat16)
-    gather_start(h_buf, sems_h, 3)
+    gather_start(h_buf, sems_h, TREES)
     send_all(n, lambda to: count.at[me], count.at[me], count_send, count_recv)
     two = acc.at[0:hidden]
 
@@ -269,14 +281,14 @@
         aggregate(two, take_two(0, 1))
         load_two(0, 1)
     with jax.named_scope('arrive'):
-        gather_arrive(h_buf, sems_h, 1, 3)
+        gather_arrive(h_buf, sems_h, 1, TREES)
     with jax.named_scope('consume'):
         aggregate(two, take_two(1, 0))
         load_two(1, 0)
 
     for p in range(2, STEPS):
         with jax.named_scope('arrive'):
-            gather_arrive(h_buf, sems_h, early_order(p), 3)
+            gather_arrive(h_buf, sems_h, early_order(p), TREES)
             gather_take(h_buf, sems_h, early_order(p - 1))
         with jax.named_scope('consume'):
             aggregate(two, take_two(p - 1, 1) + take_two(p, 0))
@@ -319,7 +331,8 @@
         return remote(stage.at[s, t], total.at[s, t], dsend, drecv.at[s], partner)
 
     def to_parent(s, t, k):
-        return remote(total.at[s, t], child.at[s - 1, t], csend, crecv.at[s - 1, t], neighbour(t, k, core, chip))
+        got = crecv.at[s + 8] if k == 2 else crecv.at[(s - 1) * TREES + t]
+        return remote(total.at[s, t], child.at[s - 1, t], csend, got, neighbour(t, k, core, chip))
 
     def reduce_small():
         @pl.when(me < owners)
@@ -350,7 +363,7 @@
 
     def from_far_to(which):
         rows, k = ((slice(0, edge_row), 2), (slice(edge_row, hidden), 1))[which]
-        sem = cut_sem if which else crecv.at[far - 1, TREES - 1]
+        sem = cut_sem.at[which]
         return remote(total.at[far, TREES - 1, rows], child.at[far - 1, TREES - 1, rows], csend, sem, neighbour(TREES - 1, k, core, chip))
 
     def add_far(s, which):
@@ -375,10 +388,17 @@
         total[s, t] = total[s, t] + mine[t]
         for k in range(3):
             skip = far - 4 if k == 2 and t == TREES - 1 else STEPS
+            if k == 2 and t == 0:
+                for few, here in ((TREES, (s < 4) & (s != far - 4)), (TREES - 1, s == far - 4)):
+                    @pl.when(here)
+                    def _():
+                        some = child.at[0, pl.ds(0, few)]
+                        remote(some, some, csend, crecv.at[s + 12], partner).wait_recv()
 
             @pl.when((s < 2 ** k) & (s != skip))
             def _():
-                to_parent(s + 2 ** k, t, k).wait_recv()
+                if k < 2:
+                    to_parent(s + 2 ** k, t, k).wait_recv()
                 total[s, t] = total[s, t] + child[s + 2 ** k - 1, t]
         if t == TREES - 1:
             for which, parent in ((0, far - 4), (1, far - 2)):
@@ -449,7 +469,7 @@
         gather_drain(buf, sems_x)
         gather_drain(h_buf, sems_h)
         remote(stage, stage, dsend, drecv.at[0], partner).wait_send()
-        remote(child, child, csend, crecv.at[0, 0], partner).wait_send()
+        remote(child, child, csend, crecv.at[0], partner).wait_send()
     with jax.named_scope('pair'):
         over.wait()
         pair[...] = pair[...] + part[mine_rows]
@@ -510,7 +530,7 @@
             pltpu.VMEM((n * share, hidden), f32), pltpu.VMEM((n // 2, share, hidden), f32), pltpu.VMEM((n * share, hidden), f32),
             pltpu.VMEM((n, 8, hidden), f32), pltpu.VMEM((small, hidden), f32), pltpu.VMEM((n // 2 * share, hidden), f32),
             pltpu.VMEM((classes, rows), bf16), pltpu.VMEM((hidden, rows), bf16), pltpu.VMEM((1, rows), f32),
-            dma((RING, 2)), dma, dma, dma, dma, dma, dma((STEPS,)), dma, dma((STEPS - 1, TREES)), *[dma] * 13, *gather_sems(), *gather_sems()],
+            dma((RING, 2)), dma, dma, dma, dma, dma, dma((STEPS,)), dma, dma((16,)), *[dma] * 12, dma((2,)), *gather_sems(), *gather_sems()],
         compiler_params=pltpu.CompilerParams(collective_id=0, has_side_effects=True, vmem_limit_bytes=62000000),
         cost_estimate=pl.CostEstimate(flops=2 * rows * nodes * (feats + 2 * hidden), bytes_accessed=6 * rows * nodes, transcendentals=0),
     )(x_rows, w_one, w2t, labels, mask, adj)

time: 135 us -> 135 us (level)
  no operation moved by 1% of the time
where the time goes in v2:
time: 135 us
  Pallas kernels  135 us (100%)
    pallas_call x1, Pallas kernels, train_step(): pl.pallas_call(functools.partial(step_kernel, n), name='step', out_shape=...  134 us

profile of v2, /device:TPU:0, one launch (start us, length us, event | category | flops | bytes accessed | tf_op | source)
XLA Modules:
  0.0 135.2 jit_solution(5216036217889902626)
XLA Ops:
  0.6 133.8 %step.1 = (f32[8,128]{1,0:T(8,128)S(1)}, f32[602,128]{1,0:T(8,128)S(1)}, f32[41,128]{1,0:T(8,128)S(1)}) custom-call(bf16[602,1024]{1,0:T(8,128)(2,1)} %bitcast.6, f32[602,128]{1,0:T(8,128)} %w_hbm.1, f32[41,128]{1,0:T(8,128)} %bitcast.7, s32[1,1024]{1,0:T(1,128)} %bitcast.9, s32[1,1024]{1,0:T(1,128)} %bitcast.10, bf16[1024,16384]{1,0:T(8,128)(2,1)} %adj.1), custom_call_target="tpu_custom_call" | custom-call | flops 28789702656 | bytes 100663296 | tf_op jit(solution)/shard_map/step/pallas_call | solution.py:519
  134.5 0.7 finish.1

commit v3 on v1

--- a/solution.py
+++ b/solution.py
@@ -156,9 +156,9 @@
     copy.wait_recv()
 
 
-def step_kernel(n, x_ref, w_hbm, w2t_ref, y_ref, m_ref, adj, loss_ref, dw_ref, dw2_ref,
+def step_kernel(n, x_ref, w_hbm, w2t_hbm, y_hbm, m_hbm, adj, loss_ref, dw_ref, dw2_ref,
                 ring, buf, acc, h_buf, s_one, z_one, u_two, w_v, small, count, stage, mine, total, child, part, parts, whole,
-                small_parts, small_whole, pair, g_two, g_one, picked,
+                small_parts, small_whole, pair, g_two, g_one, picked, w2t_ref, y_ref, m_ref,
                 ring_sem, x_sem, w_sem, count_send, count_recv, dsend, drecv, csend, crecv, fsend, frecv, gsend, grecv,
                 ssend, srecv, bsend, brecv, psend, precv, qsend, qrecv, cut_sem, *sems):
     me, core, chip, partner = place()
@@ -184,14 +184,13 @@
         fetch = [pltpu.make_async_copy(x_ref.at[:, pl.ds(t * width, width)], buf.at[me * TREES + t], x_sem) for t in range(TREES)]
         for copy in fetch:
             copy.start()
-        weight = m_ref[...].astype(jnp.float32)
-        count[me] = jnp.broadcast_to(jnp.sum(weight, axis=1, keepdims=True), count.shape[1:])
         barrier_near()
         four = buf.at[pl.ds(0, TREES)]
         pltpu.make_async_copy(four, four, x_sem).wait()
     gather_start(buf, sems_x, 2)
-    weights = pltpu.make_async_copy(w_hbm, w_v, w_sem)
-    weights.start()
+    params = [pltpu.make_async_copy(src, dst, w_sem.at[i]) for i, (src, dst) in enumerate(((w_hbm, w_v), (w2t_hbm, w2t_ref), (y_hbm, y_ref), (m_hbm, m_ref)))]
+    for copy in params:
+        copy.start()
     for s in range(RING):
         for half in range(2):
             load(s, s, half)
@@ -238,7 +237,8 @@
     for half in range(2):
         load(early_order(final - RING), slot, half)
     with jax.named_scope('mid'):
-        weights.wait()
+        for copy in params:
+            copy.wait()
         s_one[0:feats] = acc[...].astype(jnp.bfloat16)
         s_one[feats:] = jnp.zeros_like(s_one[feats:])
         w_rows = w_v[...].astype(jnp.bfloat16)
@@ -247,6 +247,8 @@
             z_one[:, cols] = z
             h_buf[me * TREES + t] = jnp.maximum(z, 0.0).astype(jnp.bfloat16)
     gather_start(h_buf, sems_h, 3)
+    weight = m_ref[...].astype(jnp.float32)
+    count[me] = jnp.broadcast_to(jnp.sum(weight, axis=1, keepdims=True), count.shape[1:])
     send_all(n, lambda to: count.at[me], count.at[me], count_send, count_recv)
     two = acc.at[0:hidden]
 
@@ -500,7 +502,7 @@
         functools.partial(step_kernel, n),
         name='step',
         out_shape=(pltpu.VMEM((8, hidden), f32), pltpu.VMEM((feats, hidden), f32), pltpu.VMEM((classes, hidden), f32)),
-        in_specs=[hbm, hbm, vmem, vmem, vmem, hbm],
+        in_specs=[hbm] * 6,
         out_specs=(vmem,) * 3,
         scratch_shapes=[
             pltpu.VMEM((RING * 8, rows, width), bf16), pltpu.VMEM((units, feats, width), bf16), pltpu.VMEM((feats, rows), f32),
@@ -510,10 +512,11 @@
             pltpu.VMEM((n * share, hidden), f32), pltpu.VMEM((n // 2, share, hidden), f32), pltpu.VMEM((n * share, hidden), f32),
             pltpu.VMEM((n, 8, hidden), f32), pltpu.VMEM((small, hidden), f32), pltpu.VMEM((n // 2 * share, hidden), f32),
             pltpu.VMEM((classes, rows), bf16), pltpu.VMEM((hidden, rows), bf16), pltpu.VMEM((1, rows), f32),
-            dma((RING, 2)), dma, dma, dma, dma, dma, dma((STEPS,)), dma, dma((STEPS - 1, TREES)), *[dma] * 13, *gather_sems(), *gather_sems()],
+            pltpu.VMEM((classes, hidden), f32), pltpu.VMEM((1, rows), jnp.int32), pltpu.VMEM((1, rows), jnp.int32),
+            dma((RING, 2)), dma, dma((4,)), dma, dma, dma, dma((STEPS,)), dma, dma((STEPS - 1, TREES)), *[dma] * 13, *gather_sems(), *gather_sems()],
         compiler_params=pltpu.CompilerParams(collective_id=0, has_side_effects=True, vmem_limit_bytes=62000000),
         cost_estimate=pl.CostEstimate(flops=2 * rows * nodes * (feats + 2 * hidden), bytes_accessed=6 * rows * nodes, transcendentals=0),
-    )(x_rows, w_one, w2t, labels, mask, adj)
+    )(*[pltpu.with_memory_space_constraint(x, pltpu.HBM) for x in (x_rows, w_one, w2t, labels, mask, adj)])
     return pl.pallas_call(
         finish_kernel,
         name='finish',

time: 135 us -> 134 us (level)
  no operation moved by 1% of the time
where the time goes in v3:
time: 134 us
  Pallas kernels  134 us (100%)
    pallas_call x1, Pallas kernels, train_step(): pl.pallas_call(functools.partial(step_kernel, n), name='step', out_shape=...  133 us

profile of v3, /device:TPU:0, one launch (start us, length us, event | category | flops | bytes accessed | tf_op | source)
XLA Modules:
  0.0 134.2 jit_solution(694210858814666219)
XLA Ops:
  0.6 132.8 %step.1 = (f32[8,128]{1,0:T(8,128)S(1)}, f32[602,128]{1,0:T(8,128)S(1)}, f32[41,128]{1,0:T(8,128)S(1)}) custom-call(bf16[602,1024]{1,0:T(8,128)(2,1)} %bitcast.6, f32[602,128]{1,0:T(8,128)} %w_hbm.1, f32[41,128]{1,0:T(8,128)} %bitcast.7, s32[1,1024]{1,0:T(1,128)} %bitcast.9, s32[1,1024]{1,0:T(1,128)} %bitcast.10, bf16[1024,16384]{1,0:T(8,128)(2,1)} %adj.1), custom_call_target="tpu_custom_call" | custom-call | flops 28789702656 | bytes 100663296 | tf_op jit(solution)/shard_map/step/pallas_call | solution.py:501
  133.5 0.7 finish.1

commit v4 on v3

--- a/solution.py
+++ b/solution.py
@@ -36,6 +36,11 @@
 def early_order(place):
     pair = (place + 1) // 2
     return place + (pair * (4 - pair)) // 4 * (7 - 2 * place)
+
+
+def other_chips(chip):
+    for flips in ((1, 2, 4), (1, 4), (1, 2), (2, 4), (1,), (2,), (4,)):
+        yield chip + sum(w * (1 - 2 * lax.rem(chip // w, 2)) for w in flips)
 
 
 def unit_at(tree, offset, core, chip):
@@ -459,16 +464,15 @@
     def share_of(q):
         return pl.ds(pl.multiple_of(q * share, 8), share)
 
-    for i in range(1, chips):
-        to = lax.rem(chip + i, chips)
+    for to in other_chips(chip):
         remote(pair.at[share_of(to)], parts.at[chip], fsend, frecv, to * 2 + core).start()
     parts[chip] = pair[share_of(chip)]
     with jax.named_scope('red'):
         wait_all(parts.at[pl.ds(0, chips - 1)], fsend, frecv)
     own = whole.at[pl.ds(pl.multiple_of(core * half + chip * share, 8), share)]
     own[...] = jnp.sum(parts[...], axis=0)
-    for i in range(1, chips):
-        remote(own, own, gsend, grecv, lax.rem(chip + i, chips) * 2 + core).start()
+    for to in other_chips(chip):
+        remote(own, own, gsend, grecv, to * 2 + core).start()
     with jax.named_scope('spread'):
         wait_all(whole.at[pl.ds(0, (chips - 1) * share)], gsend, grecv)
     swap = remote(whole.at[mine_rows], whole.at[mine_rows], qsend, qrecv, partner)

time: 134 us -> 134 us (level)
  no operation moved by 1% of the time
where the time goes in v4:
time: 134 us
  Pallas kernels  133 us (99%)
    pallas_call x1, Pallas kernels, train_step(): pl.pallas_call(functools.partial(step_kernel, n), name='step', out_shape=...  132 us

profile of v4, /device:TPU:0, one launch (start us, length us, event | category | flops | bytes accessed | tf_op | source)
XLA Modules:
  0.0 133.8 jit_solution(824084536329326641)
XLA Ops:
  0.6 132.4 %step.1 = (f32[8,128]{1,0:T(8,128)S(1)}, f32[602,128]{1,0:T(8,128)S(1)}, f32[41,128]{1,0:T(8,128)S(1)}) custom-call(bf16[602,1024]{1,0:T(8,128)(2,1)} %bitcast.6, f32[602,128]{1,0:T(8,128)} %w_hbm.1, f32[41,128]{1,0:T(8,128)} %bitcast.7, s32[1,1024]{1,0:T(1,128)} %bitcast.9, s32[1,1024]{1,0:T(1,128)} %bitcast.10, bf16[1024,16384]{1,0:T(8,128)(2,1)} %adj.1), custom_call_target="tpu_custom_call" | custom-call | flops 28789702656 | bytes 100663296 | tf_op jit(solution)/shard_map/step/pallas_call | solution.py:505
  133.0 0.7 finish.1

commit v5 on v4

--- a/solution.py
+++ b/solution.py
@@ -511,7 +511,7 @@
         scratch_shapes=[
             pltpu.VMEM((RING * 8, rows, width), bf16), pltpu.VMEM((units, feats, width), bf16), pltpu.VMEM((feats, rows), f32),
             pltpu.VMEM((units, hidden, width), bf16), pltpu.VMEM((n * share, rows), bf16), pltpu.VMEM((hidden, rows), f32),
-            pltpu.VMEM((hidden, rows), bf16), pltpu.VMEM((feats, hidden), f32), pltpu.VMEM((small, hidden), f32), pltpu.VMEM((n, 8, 128), f32),
+            pltpu.VMEM((hidden, rows), bf16), pltpu.VMEM((feats, hidden), f32), pltpu.VMEM((small, hidden), f32), pltpu.VMEM((n, 1, 128), f32),
             pltpu.VMEM((STEPS, *block), f32), pltpu.VMEM(block, f32), pltpu.VMEM((STEPS, *block), f32), pltpu.VMEM((STEPS - 1, *block), f32),
             pltpu.VMEM((n * share, hidden), f32), pltpu.VMEM((n // 2, share, hidden), f32), pltpu.VMEM((n * share, hidden), f32),
             pltpu.VMEM((n, 8, hidden), f32), pltpu.VMEM((small, hidden), f32), pltpu.VMEM((n // 2 * share, hidden), f32),

time: 134 us -> 133 us (level)
  no operation moved by 1% of the time
where the time goes in v5:
time: 133 us
  Pallas kernels  133 us (100%)
    pallas_call x1, Pallas kernels, train_step(): pl.pallas_call(functools.partial(step_kernel, n), name='step', out_shape=...  132 us

profile of v5, /device:TPU:0, one launch (start us, length us, event | category | flops | bytes accessed | tf_op | source)
XLA Modules:
  0.0 133.3 jit_solution(11103269465848623647)
XLA Ops:
  0.6 131.9 %step.1 = (f32[8,128]{1,0:T(8,128)S(1)}, f32[602,128]{1,0:T(8,128)S(1)}, f32[41,128]{1,0:T(8,128)S(1)}) custom-call(bf16[602,1024]{1,0:T(8,128)(2,1)} %bitcast.6, f32[602,128]{1,0:T(8,128)} %w_hbm.1, f32[41,128]{1,0:T(8,128)} %bitcast.7, s32[1,1024]{1,0:T(1,128)} %bitcast.9, s32[1,1024]{1,0:T(1,128)} %bitcast.10, bf16[1024,16384]{1,0:T(8,128)(2,1)} %adj.1), custom_call_target="tpu_custom_call" | custom-call | flops 28789702656 | bytes 100663296 | tf_op jit(solution)/shard_map/step/pallas_call | solution.py:505
  132.5 0.7 finish.1

commit v6 on v5

--- a/solution.py
+++ b/solution.py
@@ -367,10 +367,11 @@
 
     def give(s, slot):
         loaded(slot, 1)
-        for t in range(TREES):
-            stage[s, t] = jnp.dot(u_two[...], ring[slot * 8 + TREES + t], preferred_element_type=jnp.float32)
-        for t in range(TREES):
-            to_partner(s, t).start()
+        for two_trees in (range(TREES // 2), range(TREES // 2, TREES)):
+            for t in two_trees:
+                stage[s, t] = jnp.dot(u_two[...], ring[slot * 8 + TREES + t], preferred_element_type=jnp.float32)
+            for t in two_trees:
+                to_partner(s, t).start()
         loaded(slot, 0)
         for t in range(TREES):
             mine[t] = jnp.dot(u_two[...], ring[slot * 8 + t], preferred_element_type=jnp.float32)

time: 133 us -> 133 us (level)
  no operation moved by 1% of the time
where the time goes in v6:
time: 133 us
  Pallas kernels  133 us (100%)
    pallas_call x1, Pallas kernels, train_step(): pl.pallas_call(functools.partial(step_kernel, n), name='step', out_shape=...  132 us

profile of v6, /device:TPU:0, one launch (start us, length us, event | category | flops | bytes accessed | tf_op | source)
XLA Modules:
  0.0 133.3 jit_solution(5067946519775662640)
XLA Ops:
  0.6 131.9 %step.1 = (f32[8,128]{1,0:T(8,128)S(1)}, f32[602,128]{1,0:T(8,128)S(1)}, f32[41,128]{1,0:T(8,128)S(1)}) custom-call(bf16[602,1024]{1,0:T(8,128)(2,1)} %bitcast.6, f32[602,128]{1,0:T(8,128)} %w_hbm.1, f32[41,128]{1,0:T(8,128)} %bitcast.7, s32[1,1024]{1,0:T(1,128)} %bitcast.9, s32[1,1024]{1,0:T(1,128)} %bitcast.10, bf16[1024,16384]{1,0:T(8,128)(2,1)} %adj.1), custom_call_target="tpu_custom_call" | custom-call | flops 28789702656 | bytes 100663296 | tf_op jit(solution)/shard_map/step/pallas_call | solution.py:506
  132.6 0.7 finish.1

commit v7 on v5

--- a/solution.py
+++ b/solution.py
@@ -283,7 +283,7 @@
 
     for p in range(2, STEPS):
         with jax.named_scope('arrive'):
-            gather_arrive(h_buf, sems_h, early_order(p), 3)
+            gather_arrive(h_buf, sems_h, early_order(p), 3, cut=hidden * 2 // 3 // 16 * 16)
             gather_take(h_buf, sems_h, early_order(p - 1))
         with jax.named_scope('consume'):
             aggregate(two, take_two(p - 1, 1) + take_two(p, 0))

time: 133 us -> 134 us (level)
  no operation moved by 1% of the time
where the time goes in v7:
time: 134 us
  Pallas kernels  133 us (99%)
    pallas_call x1, Pallas kernels, train_step(): pl.pallas_call(functools.partial(step_kernel, n), name='step', out_shape=...  132 us

profile of v7, /device:TPU:0, one launch (start us, length us, event | category | flops | bytes accessed | tf_op | source)
XLA Modules:
  0.0 133.6 jit_solution(6702029477131770)
XLA Ops:
  0.6 132.2 %step.1 = (f32[8,128]{1,0:T(8,128)S(1)}, f32[602,128]{1,0:T(8,128)S(1)}, f32[41,128]{1,0:T(8,128)S(1)}) custom-call(bf16[602,1024]{1,0:T(8,128)(2,1)} %bitcast.6, f32[602,128]{1,0:T(8,128)} %w_hbm.1, f32[41,128]{1,0:T(8,128)} %bitcast.7, s32[1,1024]{1,0:T(1,128)} %bitcast.9, s32[1,1024]{1,0:T(1,128)} %bitcast.10, bf16[1024,16384]{1,0:T(8,128)(2,1)} %adj.1), custom_call_target="tpu_custom_call" | custom-call | flops 28789702656 | bytes 100663296 | tf_op jit(solution)/shard_map/step/pallas_call | solution.py:505
  132.8 0.7 finish.1
